TPU v7x, 512 devices: a whole 4x8x8 slice. The times are simulated.
512 devices in a mesh: pair: 2 (over y_lo), dp: 32 (over x, z), ep: 8 (over y_hi, core).
Axes of the slice: x: 4, y: 8 (y_hi: 4, y_lo: 2; y = y_hi * 2 + y_lo), z: 8, core: 2. Of those that a mesh axis runs over, the one named last changes fastest.
Arguments:
- activations: bfloat16 [49152, 4096], P(('pair', 'dp'), 'ep'), parts along dimension 1, may hold values from -16 to 16
- cotangents: bfloat16 [49152, 16384], P(('pair', 'dp'), 'ep'), parts along dimension 1, may hold values from -1.75 to 1.75
Outputs:
- averaged_grad: bfloat16 [512, 16384], P('pair', 'ep'), parts along dimension 1
There are 8 independent parts, one for each index of `ep`. A program takes and returns all parts, laid end to end along the dimension named above; each array names one. Nothing has to cross between parts.
All inputs are finite; a program needn't handle non-finite values.
Results may differ from a plain program's by a relative error of at most 0.001.
Values may be sent and summed in bfloat16 or wider, within the bound.
No kernel may reach another device: no remote copies, remote signals or barrier semaphores. Data moves between devices by JAX's collectives and lax.ppermute only.
A program may use at most 64 MiB of HBM per device.

v0:
```python
import jax
import jax.numpy as jnp
from jax import lax
from jax.sharding import Mesh
from jax.sharding import PartitionSpec as P

DP = ("dp_0", "dp_1")
PAIR_DP = ("pair", "dp_0", "dp_1")


def rows_for(lines, peers):
    spare = -len(lines) % peers
    return jnp.pad(lines, [(0, spare)] + [(0, 0)] * (lines.ndim - 1))


def copy_for_each(x, axis):
    copies = jnp.broadcast_to(x, (lax.axis_size(axis), *x.shape))
    return lax.all_to_all(copies, axis, split_axis=0, concat_axis=0, tiled=True)


def in_order(parts, dim):
    parts = jnp.moveaxis(parts, 0, dim)
    shape = parts.shape
    return parts.reshape(*shape[:dim], shape[dim] * shape[dim + 1], *shape[dim + 2 :])


def gathered_by_axis(x, axes, dim):
    far, near = axes
    leading = copy_for_each(x, far)
    parts = jnp.swapaxes(copy_for_each(leading, near), 0, 1)
    return in_order(parts.reshape(-1, *x.shape), dim)


def split_up(x, dim, peers):
    shape = x.shape
    parts = x.reshape(*shape[:dim], peers, shape[dim] // peers, *shape[dim + 1 :])
    return jnp.moveaxis(parts, dim, 0)


def summed_on_arrival(x, axis, dim):
    peers = lax.axis_size(axis)
    parts = lax.all_to_all(split_up(x, dim, peers), axis, 0, 0, tiled=True)
    return jnp.sum(parts, axis=0)


def sum_by_axis(x, axes, dim):
    far, near = axes
    parts = split_up(x, dim, lax.axis_size(far))
    nearer = summed_on_arrival(parts, near, dim + 1)
    arrived = lax.all_to_all(nearer, far, split_axis=0, concat_axis=0, tiled=True)
    return arrived.sum(axis=0)


def nested_sum(x, axes):
    lines = x.reshape(-1, x.shape[-1])
    padded = rows_for(lines, lax.axis_size(axes[0]) * lax.axis_size(axes[1]))
    whole = gathered_by_axis(sum_by_axis(padded, axes, 0), axes, 0)
    return lax.slice_in_dim(whole, 0, len(lines)).reshape(x.shape)


def local(activations, cotangents):
    replicas = lax.axis_size("pair") * lax.axis_size(DP)
    partial_grad = lax.dot_general(
        activations, cotangents, (((0,), (0,)), ((), ())), preferred_element_type=jnp.float32
    )
    grad_total = nested_sum(partial_grad, ("pair", ("dp_0", "dp_1")))
    half_rows = activations.shape[1] // lax.axis_size("pair")
    own_rows = lax.dynamic_slice_in_dim(
        grad_total, lax.axis_index("pair") * half_rows, half_rows, 0
    )
    return (own_rows / replicas).astype(jnp.bfloat16)


def solution(mesh):
    split = Mesh(
        mesh.devices.reshape(mesh.shape["pair"], 4, 8, mesh.shape["ep"]),
        ("pair", "dp_0", "dp_1", "ep"),
    )
    placed = (P(PAIR_DP, "ep"), P(PAIR_DP, "ep"))
    return jax.shard_map(
        local, mesh=split, in_specs=placed, out_specs=P("pair", "ep"), check_vma=False
    )
```

profile of v0, /device:TPU:48, one launch (start us, length us, event | category | flops | bytes accessed | tf_op | source)
XLA Modules:
  0.0 236.1 jit_solution(15673615468565433974)
XLA Ops:
  0.0 0.0 copy-start
  0.0 1.9 copy-done
  1.9 3.0 %fusion = f32[512,2048]{1,0:T(8,128)S(1)} fusion(bf16[768,512]{1,0:T(8,128)(2,1)} %param.2, bf16[768,2048]{1,0:T(8,128)(2,1)S(1)} %copy-done), kind=kOutput, calls=%fused_computation.2 | convolution fusion | flops 1610612736 | bytes 8126464 | tf_op jit(solution)/shard_map/dot_general | solution.py:63
  4.9 0.5 copy.9
  5.3 109.2 %all_to_all.20 = f32[32,2,8,2048]{3,2,1,0:T(8,128)} all-to-all(f32[32,2,8,2048]{3,2,1,0:T(8,128)S(1)} %bitcast.9), channel_id=1, replica_groups=mesh['pair'=2,'dp_0'=4,'dp_1'=8,'ep'=8] {'dp_0','dp_1'}, dimensions={0} | all-to-all | bytes 8388608 | tf_op jit(solution)/shard_map/all_to_all | solution.py:42
  114.6 2.4 %reduce_sum.18 = f32[2,8,2048]{2,1,0:T(8,128)S(1)} reduce(f32[32,2,8,2048]{3,2,1,0:T(8,128)} %all_to_all.20, f32[]{:T(128)} %constant.3.clone.1), dimensions={0}, to_apply=%region_0.1 | reduce | flops 1015808 | bytes 4325380 | tf_op jit(solution)/shard_map/reduce_sum | solution.py:43
  117.0 7.5 %all_to_all.21 = f32[2,8,2048]{2,1,0:T(8,128)S(1)} all-to-all(f32[2,8,2048]{2,1,0:T(8,128)S(1)} %reduce_sum.18), channel_id=1, replica_groups=mesh['pair'=2,'dp_0'=4,'dp_1'=8,'ep'=8] {'pair'}, dimensions={0} | all-to-all | bytes 262144 | tf_op jit(solution)/shard_map/all_to_all | solution.py:50
  124.5 6.8 %all_to_all.22 = f32[2,8,2048]{2,1,0:T(8,128)S(1)} all-to-all(f32[2,8,2048]{2,1,0:T(8,128)S(1)} %broadcast_in_dim.6), channel_id=1, replica_groups=mesh['pair'=2,'dp_0'=4,'dp_1'=8,'ep'=8] {'pair'}, dimensions={0} | all-to-all | bytes 262144 | tf_op jit(solution)/shard_map/all_to_all | solution.py:18
  131.3 2.5 %broadcast_in_dim.7 = f32[32,2,8,2048]{3,2,1,0:T(8,128)} broadcast(f32[2,8,2048]{2,1,0:T(8,128)S(1)} %all_to_all.22), dimensions={1,2,3} | broadcast | bytes 4325376 | tf_op jit(solution)/shard_map/broadcast_in_dim | solution.py:17
  133.8 4.8 %all-to-all-start.3 = ((f32[32,2,8,2048]{3,2,1,0:T(8,128)}), f32[32,2,8,2048]{3,2,1,0:T(8,128)}, u32[]{:S(2)}, u32[]{:S(2)}) async-start(f32[32,2,8,2048]{3,2,1,0:T(8,128)} %broadcast_in_dim.7), calls=%async_computation.3 | async-start | bytes 8388608 | tf_op jit(solution)/shard_map/all_to_all | solution.py:18
  138.6 93.9 %all-to-all-done.3 = f32[32,2,8,2048]{3,2,1,0:T(8,128)} async-done(((f32[32,2,8,2048]{3,2,1,0:T(8,128)}), f32[32,2,8,2048]{3,2,1,0:T(8,128)}, u32[]{:S(2)}, u32[]{:S(2)}) %all-to-all-start.3) | async-done | bytes 4194336 | tf_op jit(solution)/shard_map/all_to_all | solution.py:18
  232.5 2.5 %copy.7 = f32[32,2,8,2048]{3,2,0,1:T(8,128)S(1)} copy(f32[32,2,8,2048]{3,2,1,0:T(8,128)} %all-to-all-done.3) | data formatting | bytes 8388608 | tf_op jit(solution)/shard_map/all_to_all | solution.py:18
  235.0 1.1 multiply_convert_fusion
  (2 shorter events, 0.0 us)
Async XLA Ops:
  0.0 1.9 copy-start
  133.8 98.7 %all-to-all-start.3 = ((f32[32,2,8,2048]{3,2,1,0:T(8,128)}), f32[32,2,8,2048]{3,2,1,0:T(8,128)}, u32[]{:S(2)}, u32[]{:S(2)}) async-start(f32[32,2,8,2048]{3,2,1,0:T(8,128)} %broadcast_in_dim.7), calls=%async_computation.3 | async-start | bytes 8388608 | tf_op jit(solution)/shard_map/all_to_all | solution.py:18
where the time goes:
time: 237 us; the launch traced here: 236 us
  blocking collectives  124 us (52%)
  waiting for transfers between devices  93.9 us (40%)
  local copies, waits for them, and re-layouts  7.32 us (3%)
  starting transfers between devices  4.85 us (2%)
  other arithmetic  3.55 us (1%)
  matrix products  2.96 us (1%)
    all_to_all x1, blocking collectives, summed_on_arrival(): parts = lax.all_to_all(split_up(x, dim, peers), axis, 0, 0, tiled=True)  109 us
    all_to_all x1, waiting for transfers between devices, copy_for_each(): return lax.all_to_all(copies, axis, split_axis=0, concat_axis=0, tiled=True)  93.9 us
    all_to_all x1, blocking collectives, sum_by_axis(): lax.all_to_all(nearer, far, split_axis=0, concat_axis=0, tiled=True)  7.47 us
    all_to_all x1, blocking collectives, copy_for_each(): return lax.all_to_all(copies, axis, split_axis=0, concat_axis=0, tiled=True)  6.85 us
    all_to_all x1, starting transfers between devices, copy_for_each(): return lax.all_to_all(copies, axis, split_axis=0, concat_axis=0, tiled=True)  4.85 us
  transfers between devices with their start and end apart: 1, of which 1 were waited for; matrix products, arithmetic and copies ran while one was open for 0% of the time, Pallas kernels for 0%

commit v1 on v0

v1 whole, which is shorter than its diff:
```python
import jax
import jax.numpy as jnp
from jax import lax
from jax.sharding import Mesh
from jax.sharding import PartitionSpec as P

NEAR = ("pair", "x", "zl")
TOKENS = ("pair", "x", "zh", "zl")
SCALE = 2.0


def copies(x, axes, peers):
    return lax.all_to_all(
        jnp.broadcast_to(x, (peers, *x.shape)), axes, split_axis=0, concat_axis=0, tiled=True
    )


def local(activations, cotangents):
    near = lax.axis_size(NEAR)
    far = lax.axis_size("zh")
    in_plane = lax.axis_size(("x", "zl"))
    replicas = near * far
    partial_grad = lax.dot_general(
        activations, cotangents, (((0,), (0,)), ((), ())), preferred_element_type=jnp.float32
    )
    rows, cols = partial_grad.shape
    sent = (partial_grad * SCALE).astype(jnp.float16).reshape(near, rows // near, cols)
    arrived = lax.all_to_all(sent, NEAR, 0, 0, tiled=True)
    near_sum = jnp.sum(arrived.astype(jnp.float32), axis=0)
    parts = lax.all_to_all(near_sum.reshape(far, -1, cols), "zh", 0, 0, tiled=True)
    total = jnp.sum(parts, axis=0)
    own = (total * (1.0 / (SCALE * replicas))).astype(jnp.bfloat16)
    block = copies(own, "zh", far).reshape(-1, cols)
    return copies(block, ("x", "zl"), in_plane).reshape(-1, cols)


def solution(mesh):
    split = Mesh(
        mesh.devices.reshape(mesh.shape["pair"], 4, 4, 2, mesh.shape["ep"]),
        ("pair", "x", "zh", "zl", "ep"),
    )
    placed = (P(TOKENS, "ep"), P(TOKENS, "ep"))
    return jax.shard_map(
        local, mesh=split, in_specs=placed, out_specs=P("pair", "ep"), check_vma=False
    )
```

time: 237 us -> 86.8 us (0.37)
  the two profiles are of different devices: /device:TPU:48 before, /device:TPU:16 now
where the time goes in v1:
time: 86.8 us; the launch traced here: 86.5 us
  blocking collectives  80.1 us (92%)
  local copies, waits for them, and re-layouts  2.98 us (3%)
  matrix products  2.96 us (3%)
    all_to_all x1, blocking collectives, local(): arrived = lax.all_to_all(sent, NEAR, 0, 0, tiled=True)  34.2 us
    all_to_all x2, blocking collectives, copies(): lax.all_to_all(jnp.broadcast_to(x, (peers, *x.shape)), axes, split_axis=0...  25.9 us
    all_to_all x1, blocking collectives, local(): lax.all_to_all(near_sum.reshape(far, -1, cols), 'zh', 0, 0, tiled=True)  20 us
    dot_general x1, matrix products, local(): lax.dot_general(activations, cotangents, (((0,), (0,)), ((), ())), prefer...  2.96 us
    unnamed x3, local copies, waits for them, and re-layouts  2.86 us

profile of v1, /device:TPU:16, one launch (start us, length us, event | category | flops | bytes accessed | tf_op | source)
XLA Modules:
  0.0 86.5 jit_solution(396323180118155936)
XLA Ops:
  0.0 0.0 copy-start
  0.0 1.9 %copy-done = bf16[768,2048]{1,0:T(8,128)(2,1)S(1)} copy-done((bf16[768,2048]{1,0:T(8,128)(2,1)S(1)}, bf16[768,2048]{1,0:T(8,128)(2,1)}, u32[]{:S(2)}) %copy-start) | copy-done | bytes 3145752
  1.9 3.0 %multiply_convert_fusion = f16[512,2048]{1,0:T(8,128)(2,1)S(1)} fusion(bf16[768,512]{1,0:T(8,128)(2,1)} %param.2, bf16[768,2048]{1,0:T(8,128)(2,1)S(1)} %copy-done), kind=kOutput, calls=%fused_computation.1 | convolution fusion | flops 1612709888 | bytes 6029312 | tf_op jit(solution)/shard_map/dot_general | solution.py:23
  4.9 34.2 %all_to_all.20 = f16[16,32,2048]{2,1,0:T(8,128)(2,1)S(1)} all-to-all(f16[16,32,2048]{2,1,0:T(8,128)(2,1)S(1)} %bitcast.6), channel_id=1, replica_groups=mesh['pair'=2,'x'=4,'zh'=4,'zl'=2,'ep'=8] {'pair','x','zl'}, dimensions={0} | all-to-all | bytes 4194304 | tf_op jit(solution)/shard_map/all_to_all | solution.py:28
  39.1 0.4 convert_reduce_fusion
  39.5 20.0 %all_to_all.21 = f32[4,8,2048]{2,1,0:T(8,128)S(1)} all-to-all(f32[4,8,2048]{2,1,0:T(8,128)S(1)} %bitcast.8), channel_id=1, replica_groups=mesh['pair'=2,'x'=4,'zh'=4,'zl'=2,'ep'=8] {'zh'}, dimensions={0} | all-to-all | bytes 524288 | tf_op jit(solution)/shard_map/all_to_all | solution.py:30
  59.5 11.1 %all_to_all.22 = bf16[4,8,2048]{2,1,0:T(8,128)(2,1)S(1)} all-to-all(bf16[4,8,2048]{2,1,0:T(8,128)(2,1)S(1)} %broadcast_in_dim.6), channel_id=1, replica_groups=mesh['pair'=2,'x'=4,'zh'=4,'zl'=2,'ep'=8] {'zh'}, dimensions={0} | all-to-all | bytes 262144 | tf_op jit(solution)/shard_map/all_to_all | solution.py:13
  70.6 0.1 broadcast_in_dim.7
  70.7 14.8 %all_to_all.23 = bf16[8,32,2048]{2,1,0:T(8,128)(2,1)S(1)} all-to-all(bf16[8,32,2048]{2,1,0:T(8,128)(2,1)S(1)} %broadcast_in_dim.7), channel_id=1, replica_groups=mesh['pair'=2,'x'=4,'zh'=4,'zl'=2,'ep'=8] {'x','zl'}, dimensions={0} | all-to-all | bytes 2097152 | tf_op jit(solution)/shard_map/all_to_all | solution.py:13
  85.5 1.0 %copy.4 = bf16[256,2048]{1,0:T(8,128)(2,1)} copy(bf16[256,2048]{1,0:T(8,128)(2,1)S(1)} %bitcast.7) | data formatting | bytes 2097152
  (3 shorter events, 0.0 us)
Async XLA Ops:
  0.0 1.9 %copy-start = (bf16[768,2048]{1,0:T(8,128)(2,1)S(1)}, bf16[768,2048]{1,0:T(8,128)(2,1)}, u32[]{:S(2)}) copy-start(bf16[768,2048]{1,0:T(8,128)(2,1)} %param.3) | copy-start | bytes 9437188

commit v2 on v1

v2 whole, which is shorter than its diff:
```python
import jax
import jax.numpy as jnp
from jax import lax
from jax.sharding import Mesh
from jax.sharding import PartitionSpec as P

NEAR = ("pair", "x")
TOKENS = ("pair", "x", "z")
SCALE = 2.0


def copies(x, axis):
    peers = lax.axis_size(axis)
    return lax.all_to_all(
        jnp.broadcast_to(x, (peers, *x.shape)), axis, split_axis=0, concat_axis=0, tiled=True
    )


def local(activations, cotangents):
    near = lax.axis_size(NEAR)
    far = lax.axis_size("z")
    replicas = near * far
    partial_grad = lax.dot_general(
        activations, cotangents, (((0,), (0,)), ((), ())), preferred_element_type=jnp.float32
    )
    rows, cols = partial_grad.shape
    sent = (partial_grad * SCALE).astype(jnp.float16).reshape(near, rows // near, cols)
    arrived = lax.all_to_all(sent, NEAR, 0, 0, tiled=True)
    near_sum = jnp.sum(arrived.astype(jnp.float32), axis=0)
    parts = lax.all_to_all(near_sum.reshape(far, -1, cols), "z", 0, 0, tiled=True)
    total = jnp.sum(parts, axis=0)
    own = (total * (1.0 / (SCALE * replicas))).astype(jnp.bfloat16)
    block = copies(own, "z").reshape(-1, cols)
    return copies(block, "x").reshape(-1, cols)


def solution(mesh):
    split = Mesh(
        mesh.devices.reshape(mesh.shape["pair"], 4, 8, mesh.shape["ep"]),
        ("pair", "x", "z", "ep"),
    )
    placed = (P(TOKENS, "ep"), P(TOKENS, "ep"))
    return jax.shard_map(
        local, mesh=split, in_specs=placed, out_specs=P("pair", "ep"), check_vma=False
    )
```

time: 86.8 us -> 93.3 us (1.075)
  blocking collectives: 80.1 us -> 85.4 us
  other arithmetic: 0.41 us -> 1.55 us
    all_to_all x3, blocking collectives: 45.9 us -> 53.1 us  [the longest x2 27.1 us: copies(): lax.all_to_all(jnp.broadcast_to(x, (peers, *x.shape)), axis, split_axis=0...]
    all_to_all x1, blocking collectives: 34.2 us -> 32.3 us  [local(): arrived = lax.all_to_all(sent, NEAR, 0, 0, tiled=True)]
    reduce_sum x1, other arithmetic: 0.02 us -> 1.08 us  [local(): total = jnp.sum(parts, axis=0)]
where the time goes in v2:
time: 93.3 us; the launch traced here: 92.9 us
  blocking collectives  85.4 us (92%)
  local copies, waits for them, and re-layouts  2.99 us (3%)
  matrix products  2.96 us (3%)
  other arithmetic  1.55 us (2%)
    all_to_all x1, blocking collectives, local(): arrived = lax.all_to_all(sent, NEAR, 0, 0, tiled=True)  32.3 us
    all_to_all x2, blocking collectives, copies(): lax.all_to_all(jnp.broadcast_to(x, (peers, *x.shape)), axis, split_axis=0...  27.1 us
    all_to_all x1, blocking collectives, local(): lax.all_to_all(near_sum.reshape(far, -1, cols), 'z', 0, 0, tiled=True)  26 us
    dot_general x1, matrix products, local(): lax.dot_general(activations, cotangents, (((0,), (0,)), ((), ())), prefer...  2.96 us
    unnamed x3, local copies, waits for them, and re-layouts  2.86 us

profile of v2, /device:TPU:16, one launch (start us, length us, event | category | flops | bytes accessed | tf_op | source)
XLA Modules:
  0.0 92.9 jit_solution(3032469102191531098)
XLA Ops:
  0.0 0.0 copy-start
  0.0 1.9 %copy-done = bf16[768,2048]{1,0:T(8,128)(2,1)S(1)} copy-done((bf16[768,2048]{1,0:T(8,128)(2,1)S(1)}, bf16[768,2048]{1,0:T(8,128)(2,1)}, u32[]{:S(2)}) %copy-start) | copy-done | bytes 3145752
  1.9 3.0 %multiply_convert_fusion = f16[512,2048]{1,0:T(8,128)(2,1)S(1)} fusion(bf16[768,512]{1,0:T(8,128)(2,1)} %param.2, bf16[768,2048]{1,0:T(8,128)(2,1)S(1)} %copy-done), kind=kOutput, calls=%fused_computation.1 | convolution fusion | flops 1612709888 | bytes 6029312 | tf_op jit(solution)/shard_map/dot_general | solution.py:23
  4.9 32.3 %all_to_all.20 = f16[8,64,2048]{2,1,0:T(8,128)(2,1)S(1)} all-to-all(f16[8,64,2048]{2,1,0:T(8,128)(2,1)S(1)} %bitcast.6), channel_id=1, replica_groups=mesh['pair'=2,'x'=4,'z'=8,'ep'=8] {'pair','x'}, dimensions={0} | all-to-all | bytes 4194304 | tf_op jit(solution)/shard_map/all_to_all | solution.py:28
  37.2 0.5 convert_reduce_fusion
  37.6 26.0 %all_to_all.21 = f32[8,8,2048]{2,1,0:T(8,128)} all-to-all(f32[8,8,2048]{2,1,0:T(8,128)S(1)} %bitcast.8), channel_id=1, replica_groups=mesh['pair'=2,'x'=4,'z'=8,'ep'=8] {'z'}, dimensions={0} | all-to-all | bytes 1048576 | tf_op jit(solution)/shard_map/all_to_all | solution.py:30
  63.6 1.1 %reduce_sum.19 = f32[8,2048]{1,0:T(8,128)S(1)} reduce(f32[8,8,2048]{2,1,0:T(8,128)} %all_to_all.21, f32[]{:T(128)} %constant.1.clone.1), dimensions={0}, to_apply=%region_1.0 | reduce | flops 114688 | bytes 589828 | tf_op jit(solution)/shard_map/reduce_sum | solution.py:31
  64.7 12.9 %all_to_all.22 = bf16[8,8,2048]{2,1,0:T(8,128)(2,1)S(1)} all-to-all(bf16[8,8,2048]{2,1,0:T(8,128)(2,1)S(1)} %broadcast_in_dim.6), channel_id=1, replica_groups=mesh['pair'=2,'x'=4,'z'=8,'ep'=8] {'z'}, dimensions={0} | all-to-all | bytes 524288 | tf_op jit(solution)/shard_map/all_to_all | solution.py:14
  77.6 0.1 broadcast_in_dim.7
  77.7 14.2 %all_to_all.23 = bf16[4,64,2048]{2,1,0:T(8,128)(2,1)S(1)} all-to-all(bf16[4,64,2048]{2,1,0:T(8,128)(2,1)S(1)} %broadcast_in_dim.7), channel_id=1, replica_groups=mesh['pair'=2,'x'=4,'z'=8,'ep'=8] {'x'}, dimensions={0} | all-to-all | bytes 2097152 | tf_op jit(solution)/shard_map/all_to_all | solution.py:14
  92.0 1.0 %copy.4 = bf16[256,2048]{1,0:T(8,128)(2,1)} copy(bf16[256,2048]{1,0:T(8,128)(2,1)S(1)} %bitcast.7) | data formatting | bytes 2097152
  (2 shorter events, 0.0 us)
Async XLA Ops:
  0.0 1.9 %copy-start = (bf16[768,2048]{1,0:T(8,128)(2,1)S(1)}, bf16[768,2048]{1,0:T(8,128)(2,1)}, u32[]{:S(2)}) copy-start(bf16[768,2048]{1,0:T(8,128)(2,1)} %param.3) | copy-start | bytes 9437188

commit v3 on v1

--- a/solution.py
+++ b/solution.py
@@ -1,12 +1,31 @@
 import jax
 import jax.numpy as jnp
 from jax import lax
+from jax.experimental import pallas as pl
+from jax.experimental.pallas import tpu as pltpu
 from jax.sharding import Mesh
 from jax.sharding import PartitionSpec as P
 
 NEAR = ("pair", "x", "zl")
 TOKENS = ("pair", "x", "zh", "zl")
 SCALE = 2.0
+STAGGER_NS = 6000
+
+
+def scale_kernel(late_ns, out):
+    pl.delay(late_ns[0])
+    out[...] = jnp.full(out.shape, SCALE, out.dtype)
+
+
+def staggered_scale():
+    late_ns = (lax.axis_index("ep") % 2) * STAGGER_NS
+    return pl.pallas_call(
+        scale_kernel,
+        in_specs=[pl.BlockSpec(memory_space=pltpu.SMEM)],
+        out_specs=pl.BlockSpec(memory_space=pltpu.VMEM),
+        out_shape=jax.ShapeDtypeStruct((1, 128), jnp.float32),
+        name="staggered_scale",
+    )(late_ns.astype(jnp.int32).reshape(1))[0, 0]
 
 
 def copies(x, axes, peers):
@@ -24,7 +43,7 @@
         activations, cotangents, (((0,), (0,)), ((), ())), preferred_element_type=jnp.float32
     )
     rows, cols = partial_grad.shape
-    sent = (partial_grad * SCALE).astype(jnp.float16).reshape(near, rows // near, cols)
+    sent = (partial_grad * staggered_scale()).astype(jnp.float16).reshape(near, rows // near, cols)
     arrived = lax.all_to_all(sent, NEAR, 0, 0, tiled=True)
     near_sum = jnp.sum(arrived.astype(jnp.float32), axis=0)
     parts = lax.all_to_all(near_sum.reshape(far, -1, cols), "zh", 0, 0, tiled=True)

time: 86.8 us -> 93.5 us (1.077)
  the two profiles are of different devices: /device:TPU:16 before, /device:TPU:1 now
where the time goes in v3:
time: 93.5 us; the launch traced here: 93.2 us
  blocking collectives  81.4 us (87%)
  Pallas kernels  6.59 us (7%)
  matrix products  3.65 us (4%)
  local copies, waits for them, and re-layouts  1.09 us (1%)
    all_to_all x1, blocking collectives, local(): arrived = lax.all_to_all(sent, NEAR, 0, 0, tiled=True)  32.9 us
    all_to_all x2, blocking collectives, copies(): lax.all_to_all(jnp.broadcast_to(x, (peers, *x.shape)), axes, split_axis=0...  30.3 us
    all_to_all x1, blocking collectives, local(): lax.all_to_all(near_sum.reshape(far, -1, cols), 'zh', 0, 0, tiled=True)  18.2 us
    pallas_call x1, Pallas kernels, staggered_scale(): pl.pallas_call(scale_kernel, in_specs=[pl.BlockSpec(memory_space=pltpu.SM...  6.59 us
    dot_general x1, matrix products, local(): lax.dot_general(activations, cotangents, (((0,), (0,)), ((), ())), prefer...  3.65 us

profile of v3, /device:TPU:1, one launch (start us, length us, event | category | flops | bytes accessed | tf_op | source)
XLA Modules:
  0.0 93.2 jit_solution(1855753414373043377)
XLA Ops:
  0.0 0.0 copy-start
  0.0 6.6 %staggered_scale.1 = f32[1,128]{1,0:T(1,128)} custom-call(s32[1]{0:T(128)} %bitcast.late_ns), custom_call_target="tpu_custom_call" | custom-call | tf_op jit(solution)/shard_map/staggered_scale/pallas_call | solution.py:22
  6.6 0.0 copy-done
  6.6 3.7 %multiply_convert_fusion = f16[512,2048]{1,0:T(8,128)(2,1)S(1)} fusion(bf16[768,512]{1,0:T(8,128)(2,1)} %param.2, bf16[768,2048]{1,0:T(8,128)(2,1)S(1)} %copy-done, f32[]{:T(128)} %bitcast.13), kind=kOutput, calls=%fused_computation.1 | convolution fusion | flops 1612709888 | bytes 6029316 | tf_op jit(solution)/shard_map/dot_general | solution.py:42
  10.3 32.9 %all_to_all.20 = f16[16,32,2048]{2,1,0:T(8,128)(2,1)S(1)} all-to-all(f16[16,32,2048]{2,1,0:T(8,128)(2,1)S(1)} %bitcast.9), channel_id=1, replica_groups=mesh['pair'=2,'x'=4,'zh'=4,'zl'=2,'ep'=8] {'pair','x','zl'}, dimensions={0} | all-to-all | bytes 4194304 | tf_op jit(solution)/shard_map/all_to_all | solution.py:47
  43.1 0.4 convert_reduce_fusion
  43.5 18.2 %all_to_all.21 = f32[4,8,2048]{2,1,0:T(8,128)S(1)} all-to-all(f32[4,8,2048]{2,1,0:T(8,128)S(1)} %bitcast.11), channel_id=1, replica_groups=mesh['pair'=2,'x'=4,'zh'=4,'zl'=2,'ep'=8] {'zh'}, dimensions={0} | all-to-all | bytes 524288 | tf_op jit(solution)/shard_map/all_to_all | solution.py:49
  61.8 10.0 %all_to_all.22 = bf16[4,8,2048]{2,1,0:T(8,128)(2,1)S(1)} all-to-all(bf16[4,8,2048]{2,1,0:T(8,128)(2,1)S(1)} %broadcast_in_dim.6), channel_id=1, replica_groups=mesh['pair'=2,'x'=4,'zh'=4,'zl'=2,'ep'=8] {'zh'}, dimensions={0} | all-to-all | bytes 262144 | tf_op jit(solution)/shard_map/all_to_all | solution.py:32
  71.8 0.1 broadcast_in_dim.7
  71.9 20.3 %all_to_all.23 = bf16[8,32,2048]{2,1,0:T(8,128)(2,1)S(1)} all-to-all(bf16[8,32,2048]{2,1,0:T(8,128)(2,1)S(1)} %broadcast_in_dim.7), channel_id=1, replica_groups=mesh['pair'=2,'x'=4,'zh'=4,'zl'=2,'ep'=8] {'x','zl'}, dimensions={0} | all-to-all | bytes 2097152 | tf_op jit(solution)/shard_map/all_to_all | solution.py:32
  92.2 1.0 %copy.4 = bf16[256,2048]{1,0:T(8,128)(2,1)} copy(bf16[256,2048]{1,0:T(8,128)(2,1)S(1)} %bitcast.10) | data formatting | bytes 2097152
  (3 shorter events, 0.0 us)
Async XLA Ops:
  0.0 6.6 %copy-start = (bf16[768,2048]{1,0:T(8,128)(2,1)S(1)}, bf16[768,2048]{1,0:T(8,128)(2,1)}, u32[]{:S(2)}) copy-start(bf16[768,2048]{1,0:T(8,128)(2,1)} %param.3) | copy-start | bytes 9437188

commit v4 on v1

--- a/solution.py
+++ b/solution.py
@@ -7,12 +7,28 @@
 NEAR = ("pair", "x", "zl")
 TOKENS = ("pair", "x", "zh", "zl")
 SCALE = 2.0
+LANES = 128
+TOP = 15
 
 
 def copies(x, axes, peers):
     return lax.all_to_all(
         jnp.broadcast_to(x, (peers, *x.shape)), axes, split_axis=0, concat_axis=0, tiled=True
     )
+
+
+def coded(x):
+    largest = jnp.maximum(jnp.max(jnp.abs(x)), 2.0**-100)
+    k = jnp.ceil(jnp.log2(largest))
+    u = x * jnp.exp2(-k)
+    exponent = jnp.full((x.shape[0], LANES), k, jnp.float32)
+    return jnp.concatenate([u * u * u * 2.0**TOP, exponent], axis=1).astype(jnp.float16)
+
+
+def decoded(sent):
+    code = sent[..., :-LANES].astype(jnp.float32)
+    k = sent[..., -1:].astype(jnp.float32)
+    return jnp.sign(code) * jnp.exp2((jnp.log2(jnp.abs(code)) - TOP) * (1.0 / 3.0) + k)
 
 
 def local(activations, cotangents):
@@ -27,11 +43,9 @@
     sent = (partial_grad * SCALE).astype(jnp.float16).reshape(near, rows // near, cols)
     arrived = lax.all_to_all(sent, NEAR, 0, 0, tiled=True)
     near_sum = jnp.sum(arrived.astype(jnp.float32), axis=0)
-    parts = lax.all_to_all(near_sum.reshape(far, -1, cols), "zh", 0, 0, tiled=True)
-    total = jnp.sum(parts, axis=0)
+    total = jnp.sum(decoded(copies(coded(near_sum), "zh", far)), axis=0)
     own = (total * (1.0 / (SCALE * replicas))).astype(jnp.bfloat16)
-    block = copies(own, "zh", far).reshape(-1, cols)
-    return copies(block, ("x", "zl"), in_plane).reshape(-1, cols)
+    return copies(own, ("x", "zl"), in_plane).reshape(-1, cols)
 
 
 def solution(mesh):

time: 86.8 us -> 85.8 us (0.988)
  blocking collectives: 80.1 us -> 76.7 us
  other arithmetic: 0.41 us -> 1.93 us
    all_to_all x1 -> x0, blocking collectives: 20 us -> none  [local(): lax.all_to_all(near_sum.reshape(far, -1, cols), 'zh', 0, 0, tiled=True)]
    all_to_all x2, blocking collectives: 25.9 us -> 42.5 us  [copies(): lax.all_to_all(jnp.broadcast_to(x, (peers, *x.shape)), axes, split_axis=0...]
where the time goes in v4:
time: 85.8 us; the launch traced here: 85.5 us
  blocking collectives  76.7 us (89%)
  local copies, waits for them, and re-layouts  3.04 us (4%)
  matrix products  2.96 us (3%)
  other arithmetic  1.93 us (2%)
    all_to_all x2, blocking collectives, copies(): lax.all_to_all(jnp.broadcast_to(x, (peers, *x.shape)), axes, split_axis=0...  42.5 us
    all_to_all x1, blocking collectives, local(): arrived = lax.all_to_all(sent, NEAR, 0, 0, tiled=True)  34.2 us
    dot_general x1, matrix products, local(): lax.dot_general(activations, cotangents, (((0,), (0,)), ((), ())), prefer...  2.96 us
    unnamed x3, local copies, waits for them, and re-layouts  2.86 us

profile of v4, /device:TPU:16, one launch (start us, length us, event | category | flops | bytes accessed | tf_op | source)
XLA Modules:
  0.0 85.5 jit_solution(1372604660822103457)
XLA Ops:
  0.0 0.0 copy-start
  0.0 1.9 %copy-done = bf16[768,2048]{1,0:T(8,128)(2,1)S(1)} copy-done((bf16[768,2048]{1,0:T(8,128)(2,1)S(1)}, bf16[768,2048]{1,0:T(8,128)(2,1)}, u32[]{:S(2)}) %copy-start) | copy-done | bytes 3145752
  1.9 3.0 %multiply_convert_fusion = f16[512,2048]{1,0:T(8,128)(2,1)S(1)} fusion(bf16[768,512]{1,0:T(8,128)(2,1)} %param.2, bf16[768,2048]{1,0:T(8,128)(2,1)S(1)} %copy-done), kind=kOutput, calls=%fused_computation.1 | convolution fusion | flops 1612709888 | bytes 6029312 | tf_op jit(solution)/shard_map/dot_general | solution.py:39
  4.9 34.2 %all_to_all.15 = f16[16,32,2048]{2,1,0:T(8,128)(2,1)S(1)} all-to-all(f16[16,32,2048]{2,1,0:T(8,128)(2,1)S(1)} %bitcast.4), channel_id=1, replica_groups=mesh['pair'=2,'x'=4,'zh'=4,'zl'=2,'ep'=8] {'pair','x','zl'}, dimensions={0} | all-to-all | bytes 4194304 | tf_op jit(solution)/shard_map/all_to_all | solution.py:44
  39.1 0.4 convert_reduce_fusion
  39.5 0.6 abs_reduce_fusion
  40.8 0.1 fusion.10
  41.0 25.7 %all_to_all.16 = f16[4,32,2176]{2,1,0:T(8,128)(2,1)S(1)} all-to-all(f16[4,32,2176]{2,1,0:T(8,128)(2,1)S(1)} %broadcast_in_dim.7), channel_id=1, replica_groups=mesh['pair'=2,'x'=4,'zh'=4,'zl'=2,'ep'=8] {'zh'}, dimensions={0} | all-to-all | bytes 1114112 | tf_op jit(solution)/shard_map/all_to_all | solution.py:15
  66.6 0.2 convert_reduce_fusion.1
  66.8 0.7 fusion.1
  67.5 0.1 broadcast_in_dim.8
  67.6 16.9 %all_to_all.17 = bf16[8,32,2048]{2,1,0:T(8,128)(2,1)S(1)} all-to-all(bf16[8,32,2048]{2,1,0:T(8,128)(2,1)S(1)} %broadcast_in_dim.8), channel_id=1, replica_groups=mesh['pair'=2,'x'=4,'zh'=4,'zl'=2,'ep'=8] {'x','zl'}, dimensions={0} | all-to-all | bytes 2097152 | tf_op jit(solution)/shard_map/all_to_all | solution.py:15
  84.5 1.0 %copy.11 = bf16[256,2048]{1,0:T(8,128)(2,1)} copy(bf16[256,2048]{1,0:T(8,128)(2,1)S(1)} %bitcast.5) | data formatting | bytes 2097152
  (3 shorter events, 0.1 us)
Async XLA Ops:
  0.0 1.9 %copy-start = (bf16[768,2048]{1,0:T(8,128)(2,1)S(1)}, bf16[768,2048]{1,0:T(8,128)(2,1)}, u32[]{:S(2)}) copy-start(bf16[768,2048]{1,0:T(8,128)(2,1)} %param.3) | copy-start | bytes 9437188

commit v5 on v1

v5 whole, which is shorter than its diff:
```python
import itertools

import jax
import jax.numpy as jnp
from jax import lax
from jax.sharding import Mesh
from jax.sharding import PartitionSpec as P

SIZES = {"pair": 2, "x": 4, "zh": 4, "zl": 2}
NEAR = ("pair", "x")
ALONG_Z = ("zl", "zh")
TOKENS = ("pair", "x", "zh", "zl")
SLAB = ("yh", "core")
CORES = 2
SCALE = 2.0


def groups(axes_of_core):
    found = []
    for core, along in enumerate(axes_of_core):
        others = [axis for axis in SIZES if axis not in along]
        for rest in itertools.product(*(range(SIZES[axis]) for axis in others)):
            group = []
            for place in itertools.product(*(range(SIZES[axis]) for axis in along)):
                at = dict(zip((*others, *along), (*rest, *place)))
                index = 0
                for axis, size in SIZES.items():
                    index = index * size + at[axis]
                group.append(index * CORES + core)
            found.append(group)
    return found


def exchanged(x, axes_of_core):
    return lax.all_to_all(
        x, (*SIZES, "core"), 0, 0, axis_index_groups=groups(axes_of_core), tiled=True
    )


def copies(x, axes, peers):
    return lax.all_to_all(
        jnp.broadcast_to(x, (peers, *x.shape)), axes, split_axis=0, concat_axis=0, tiled=True
    )


def arranged(sent, near, far):
    cols = sent.shape[1]
    by_place = sent.reshape(near, far, -1, cols)
    mine = lax.axis_index("core") == 0
    return jnp.where(mine, by_place, jnp.swapaxes(by_place, 0, 1)).reshape(near, -1, cols)


def local(activations, cotangents):
    near = lax.axis_size(NEAR)
    far = lax.axis_size(ALONG_Z)
    replicas = near * far
    partial_grad = lax.dot_general(
        activations, cotangents, (((0,), (0,)), ((), ())), preferred_element_type=jnp.float32
    )
    cols = partial_grad.shape[1]
    sent = arranged((partial_grad * SCALE).astype(jnp.float16), near, far)
    first_sum = jnp.sum(exchanged(sent, (NEAR, ALONG_Z)).astype(jnp.float32), axis=0)
    parts = exchanged(first_sum.reshape(far, -1, cols), (ALONG_Z, NEAR))
    total = jnp.sum(parts, axis=0)
    own = (total * (1.0 / (SCALE * replicas))).astype(jnp.bfloat16)
    block = copies(own, "zh", lax.axis_size("zh")).reshape(-1, cols)
    return copies(block, ("x", "zl"), lax.axis_size(("x", "zl"))).reshape(-1, cols)


def solution(mesh):
    split = Mesh(
        mesh.devices.reshape(*SIZES.values(), mesh.shape["ep"] // CORES, CORES),
        (*SIZES, *SLAB),
    )
    placed = (P(TOKENS, SLAB), P(TOKENS, SLAB))
    return jax.shard_map(
        local, mesh=split, in_specs=placed, out_specs=P("pair", SLAB), check_vma=False
    )
```

time: 86.8 us -> 86 us (level)
  the two profiles are of different devices: /device:TPU:16 before, /device:TPU:1 now
where the time goes in v5:
time: 86 us; the launch traced here: 85.6 us
  blocking collectives  77.4 us (90%)
  local copies, waits for them, and re-layouts  2.98 us (3%)
  matrix products  2.96 us (3%)
  other arithmetic  2.23 us (3%)
    all_to_all x2, blocking collectives, exchanged(): lax.all_to_all(x, (*SIZES, 'core'), 0, 0, axis_index_groups=groups(axes_o...  50.6 us
    all_to_all x2, blocking collectives, copies(): lax.all_to_all(jnp.broadcast_to(x, (peers, *x.shape)), axes, split_axis=0...  26.7 us
    dot_general x1, matrix products, local(): lax.dot_general(activations, cotangents, (((0,), (0,)), ((), ())), prefer...  2.96 us
    unnamed x3, local copies, waits for them, and re-layouts  2.86 us

profile of v5, /device:TPU:1, one launch (start us, length us, event | category | flops | bytes accessed | tf_op | source)
XLA Modules:
  0.0 85.6 jit_solution(9942775720415851615)
XLA Ops:
  0.0 0.0 copy-start
  0.0 1.9 %copy-done = bf16[768,2048]{1,0:T(8,128)(2,1)S(1)} copy-done((bf16[768,2048]{1,0:T(8,128)(2,1)S(1)}, bf16[768,2048]{1,0:T(8,128)(2,1)}, u32[]{:S(2)}) %copy-start) | copy-done | bytes 3145752
  1.9 3.0 %multiply_convert_fusion = f16[512,2048]{1,0:T(8,128)(2,1)S(1)} fusion(bf16[768,512]{1,0:T(8,128)(2,1)} %param.2, bf16[768,2048]{1,0:T(8,128)(2,1)S(1)} %copy-done), kind=kOutput, calls=%fused_computation.1 | convolution fusion | flops 1612709888 | bytes 6029312 | tf_op jit(solution)/shard_map/dot_general | solution.py:57
  4.9 0.7 fusion
  5.6 38.2 %all_to_all.20 = f16[8,64,2048]{2,1,0:T(8,128)(2,1)S(1)} all-to-all(f16[8,64,2048]{2,1,0:T(8,128)(2,1)S(1)} %fusion), channel_id=1, replica_groups={{0,64,128,192,256,320,384,448},{8,72,136,200,264,328,392,456},{16,80,14..., dimensions={0} | all-to-all | bytes 4194304 | tf_op jit(solution)/shard_map/all_to_all | solution.py:35
  43.8 0.5 convert_reduce_fusion
  44.2 12.4 %all_to_all.21 = f32[8,8,2048]{2,1,0:T(8,128)} all-to-all(f32[8,8,2048]{2,1,0:T(8,128)S(1)} %bitcast.14), channel_id=1, replica_groups={{0,16,32,48,8,24,40,56},{64,80,96,112,72,88,104,120},{128,144,160,176,1..., dimensions={0} | all-to-all | bytes 1048576 | tf_op jit(solution)/shard_map/all_to_all | solution.py:35
  56.7 1.1 %reduce_sum.19 = f32[8,2048]{1,0:T(8,128)S(1)} reduce(f32[8,8,2048]{2,1,0:T(8,128)} %all_to_all.21, f32[]{:T(128)} %constant.3.clone.1), dimensions={0}, to_apply=%region_1.2 | reduce | flops 114688 | bytes 589828 | tf_op jit(solution)/shard_map/reduce_sum | solution.py:64
  57.8 11.9 %all_to_all.22 = bf16[4,8,2048]{2,1,0:T(8,128)(2,1)S(1)} all-to-all(bf16[4,8,2048]{2,1,0:T(8,128)(2,1)S(1)} %broadcast_in_dim.6), channel_id=1, replica_groups=mesh['pair'=2,'x'=4,'zh'=4,'zl'=2,'yh'=4,'core'=2] {'zh'}, dimensions={0} | all-to-all | bytes 262144 | tf_op jit(solution)/shard_map/all_to_all | solution.py:41
  69.7 0.1 broadcast_in_dim.7
  69.8 14.9 %all_to_all.23 = bf16[8,32,2048]{2,1,0:T(8,128)(2,1)S(1)} all-to-all(bf16[8,32,2048]{2,1,0:T(8,128)(2,1)S(1)} %broadcast_in_dim.7), channel_id=1, replica_groups=mesh['pair'=2,'x'=4,'zh'=4,'zl'=2,'yh'=4,'core'=2] {'x','zl'}, dimensions={0} | all-to-all | bytes 2097152 | tf_op jit(solution)/shard_map/all_to_all | solution.py:41
  84.6 1.0 %copy.7 = bf16[256,2048]{1,0:T(8,128)(2,1)} copy(bf16[256,2048]{1,0:T(8,128)(2,1)S(1)} %bitcast.13) | data formatting | bytes 2097152
  (2 shorter events, 0.0 us)
Async XLA Ops:
  0.0 1.9 %copy-start = (bf16[768,2048]{1,0:T(8,128)(2,1)S(1)}, bf16[768,2048]{1,0:T(8,128)(2,1)}, u32[]{:S(2)}) copy-start(bf16[768,2048]{1,0:T(8,128)(2,1)} %param.3) | copy-start | bytes 9437188

commit v6 on v5

--- a/solution.py
+++ b/solution.py
@@ -3,6 +3,8 @@
 import jax
 import jax.numpy as jnp
 from jax import lax
+from jax.experimental import pallas as pl
+from jax.experimental.pallas import tpu as pltpu
 from jax.sharding import Mesh
 from jax.sharding import PartitionSpec as P
 
@@ -13,6 +15,65 @@
 SLAB = ("yh", "core")
 CORES = 2
 SCALE = 2.0
+CHUNKS = 2
+
+
+def product_kernel(core, acts_hbm, cots_hbm, out, acts, cots, sems):
+    near, far, _, cols = out.shape
+    width = cols // CHUNKS
+    loads = [pltpu.make_async_copy(acts_hbm, acts, sems.at[CHUNKS])]
+    for i in range(CHUNKS):
+        chunk = pl.ds(i * width, width)
+        loads.append(pltpu.make_async_copy(cots_hbm.at[:, chunk], cots.at[:, chunk], sems.at[i]))
+    for load in loads:
+        load.start()
+
+    def multiply(arrange):
+        loads[0].wait()
+        for i in range(CHUNKS):
+            loads[i + 1].wait()
+            chunk = pl.ds(i * width, width)
+            part = lax.dot_general(
+                acts[...],
+                cots[:, chunk],
+                (((0,), (0,)), ((), ())),
+                preferred_element_type=jnp.float32,
+            )
+            out[:, :, :, chunk] = arrange(part.reshape(near, far, -1, width))
+
+    @pl.when(core[0] == 0)
+    def _():
+        multiply(lambda rows: rows)
+
+    @pl.when(core[0] != 0)
+    def _():
+        multiply(lambda rows: jnp.swapaxes(rows, 0, 1))
+
+
+def product(activations, cotangents, near, far):
+    tokens, rows = activations.shape
+    cols = cotangents.shape[1]
+    return pl.pallas_call(
+        product_kernel,
+        in_specs=[
+            pl.BlockSpec(memory_space=pltpu.SMEM),
+            pl.BlockSpec(memory_space=pltpu.HBM),
+            pl.BlockSpec(memory_space=pltpu.HBM),
+        ],
+        out_specs=pl.BlockSpec(memory_space=pltpu.VMEM),
+        out_shape=pltpu.VMEM((near, far, rows // (near * far), cols), jnp.float32),
+        scratch_shapes=[
+            pltpu.VMEM((tokens, rows), activations.dtype),
+            pltpu.VMEM((tokens, cols), cotangents.dtype),
+            pltpu.SemaphoreType.DMA((CHUNKS + 1,)),
+        ],
+        compiler_params=pltpu.CompilerParams(vmem_limit_bytes=20 * 2**20),
+        name="product",
+    )(
+        lax.axis_index("core").astype(jnp.int32).reshape(1),
+        pltpu.with_memory_space_constraint(activations, pltpu.HBM),
+        pltpu.with_memory_space_constraint(cotangents, pltpu.HBM),
+    )
 
 
 def groups(axes_of_core):
@@ -43,22 +104,13 @@
     )
 
 
-def arranged(sent, near, far):
-    cols = sent.shape[1]
-    by_place = sent.reshape(near, far, -1, cols)
-    mine = lax.axis_index("core") == 0
-    return jnp.where(mine, by_place, jnp.swapaxes(by_place, 0, 1)).reshape(near, -1, cols)
-
-
 def local(activations, cotangents):
     near = lax.axis_size(NEAR)
     far = lax.axis_size(ALONG_Z)
     replicas = near * far
-    partial_grad = lax.dot_general(
-        activations, cotangents, (((0,), (0,)), ((), ())), preferred_element_type=jnp.float32
-    )
-    cols = partial_grad.shape[1]
-    sent = arranged((partial_grad * SCALE).astype(jnp.float16), near, far)
+    cols = cotangents.shape[1]
+    partial_grad = product(activations, cotangents, near, far)
+    sent = (partial_grad * SCALE).astype(jnp.float16).reshape(near, -1, cols)
     first_sum = jnp.sum(exchanged(sent, (NEAR, ALONG_Z)).astype(jnp.float32), axis=0)
     parts = exchanged(first_sum.reshape(far, -1, cols), (ALONG_Z, NEAR))
     total = jnp.sum(parts, axis=0)

time: 86 us -> 83.4 us (0.970)
  Pallas kernels: 0 us -> 3.7 us
  matrix products: 2.96 us -> 0 us
  local copies, waits for them, and re-layouts: 2.98 us -> 1.09 us
  other arithmetic: 2.23 us -> 1.02 us
    pallas_call x0 -> x1, Pallas kernels: none -> 3.7 us  [product(): pl.pallas_call(product_kernel, in_specs=[pl.BlockSpec(memory_space=pltpu....]
    dot_general x1 -> x0, matrix products: 2.96 us -> none  [local(): lax.dot_general(activations, cotangents, (((0,), (0,)), ((), ())), prefer...]
    unnamed x3 -> x1, local copies, waits for them, and re-layouts: 2.86 us -> 0.97 us
    reduce_sum x1, other arithmetic: 1.08 us -> 0.03 us  [local(): total = jnp.sum(parts, axis=0)]
where the time goes in v6:
time: 83.4 us; the launch traced here: 83.1 us
  blocking collectives  77.3 us (93%)
  Pallas kernels  3.7 us (4%)
  local copies, waits for them, and re-layouts  1.09 us (1%)
  other arithmetic  1.02 us (1%)
    all_to_all x2, blocking collectives, exchanged(): lax.all_to_all(x, (*SIZES, 'core'), 0, 0, axis_index_groups=groups(axes_o...  50.5 us
    all_to_all x2, blocking collectives, copies(): lax.all_to_all(jnp.broadcast_to(x, (peers, *x.shape)), axes, split_axis=0...  26.8 us
    pallas_call x1, Pallas kernels, product(): pl.pallas_call(product_kernel, in_specs=[pl.BlockSpec(memory_space=pltpu....  3.7 us

profile of v6, /device:TPU:1, one launch (start us, length us, event | category | flops | bytes accessed | tf_op | source)
XLA Modules:
  0.0 83.1 jit_solution(226413125209059566)
XLA Ops:
  0.0 3.7 %product.1 = f32[8,8,8,2048]{3,2,1,0:T(8,128)S(1)} custom-call(s32[1]{0:T(128)} %bitcast.core, bf16[768,512]{1,0:T(8,128)(2,1)} %acts_hbm.1, bf16[768,2048]{1,0:T(8,128)(2,1)} %cots_hbm.1), custom_call_target="tpu_custom_call" | custom-call | tf_op jit(solution)/shard_map/product/pallas_call | solution.py:56
  3.7 0.5 fusion
  4.2 38.2 %all_to_all.20 = f16[8,64,2048]{2,1,0:T(8,128)(2,1)S(1)} all-to-all(f16[8,64,2048]{2,1,0:T(8,128)(2,1)S(1)} %fusion), channel_id=1, replica_groups={{0,64,128,192,256,320,384,448},{8,72,136,200,264,328,392,456},{16,80,14..., dimensions={0} | all-to-all | bytes 4194304 | tf_op jit(solution)/shard_map/all_to_all | solution.py:96
  42.4 0.5 convert_reduce_fusion
  42.9 12.3 %all_to_all.21 = f32[8,8,2048]{2,1,0:T(8,128)S(1)} all-to-all(f32[8,8,2048]{2,1,0:T(8,128)S(1)} %bitcast.7), channel_id=1, replica_groups={{0,16,32,48,8,24,40,56},{64,80,96,112,72,88,104,120},{128,144,160,176,1..., dimensions={0} | all-to-all | bytes 1048576 | tf_op jit(solution)/shard_map/all_to_all | solution.py:96
  55.3 11.8 %all_to_all.22 = bf16[4,8,2048]{2,1,0:T(8,128)(2,1)S(1)} all-to-all(bf16[4,8,2048]{2,1,0:T(8,128)(2,1)S(1)} %broadcast_in_dim.6), channel_id=1, replica_groups=mesh['pair'=2,'x'=4,'zh'=4,'zl'=2,'yh'=4,'core'=2] {'zh'}, dimensions={0} | all-to-all | bytes 262144 | tf_op jit(solution)/shard_map/all_to_all | solution.py:102
  67.1 0.1 broadcast_in_dim.7
  67.2 15.0 %all_to_all.23 = bf16[8,32,2048]{2,1,0:T(8,128)(2,1)S(1)} all-to-all(bf16[8,32,2048]{2,1,0:T(8,128)(2,1)S(1)} %broadcast_in_dim.7), channel_id=1, replica_groups=mesh['pair'=2,'x'=4,'zh'=4,'zl'=2,'yh'=4,'core'=2] {'x','zl'}, dimensions={0} | all-to-all | bytes 2097152 | tf_op jit(solution)/shard_map/all_to_all | solution.py:102
  82.2 1.0 %copy.4 = bf16[256,2048]{1,0:T(8,128)(2,1)} copy(bf16[256,2048]{1,0:T(8,128)(2,1)S(1)} %bitcast.6) | data formatting | bytes 2097152
  (3 shorter events, 0.0 us)

commit v7 on v6

--- a/solution.py
+++ b/solution.py
@@ -16,6 +16,7 @@
 CORES = 2
 SCALE = 2.0
 CHUNKS = 2
+LATER_NS = 3000
 
 
 def product_kernel(core, acts_hbm, cots_hbm, out, acts, cots, sems):
@@ -43,6 +44,7 @@
 
     @pl.when(core[0] == 0)
     def _():
+        pl.delay(LATER_NS)
         multiply(lambda rows: rows)
 
     @pl.when(core[0] != 0)

time: 83.4 us -> 84.3 us (1.011)
  blocking collectives: 77.3 us -> 78.2 us
where the time goes in v7:
time: 84.3 us; the launch traced here: 84.1 us
  blocking collectives  78.2 us (93%)
  Pallas kernels  3.7 us (4%)
  local copies, waits for them, and re-layouts  1.09 us (1%)
  other arithmetic  1.02 us (1%)
    all_to_all x2, blocking collectives, exchanged(): lax.all_to_all(x, (*SIZES, 'core'), 0, 0, axis_index_groups=groups(axes_o...  50.7 us
    all_to_all x2, blocking collectives, copies(): lax.all_to_all(jnp.broadcast_to(x, (peers, *x.shape)), axes, split_axis=0...  27.5 us
    pallas_call x1, Pallas kernels, product(): pl.pallas_call(product_kernel, in_specs=[pl.BlockSpec(memory_space=pltpu....  3.7 us

profile of v7, /device:TPU:1, one launch (start us, length us, event | category | flops | bytes accessed | tf_op | source)
XLA Modules:
  0.0 84.1 jit_solution(11681117833216049545)
XLA Ops:
  0.0 3.7 %product.1 = f32[8,8,8,2048]{3,2,1,0:T(8,128)S(1)} custom-call(s32[1]{0:T(128)} %bitcast.core, bf16[768,512]{1,0:T(8,128)(2,1)} %acts_hbm.1, bf16[768,2048]{1,0:T(8,128)(2,1)} %cots_hbm.1), custom_call_target="tpu_custom_call" | custom-call | tf_op jit(solution)/shard_map/product/pallas_call | solution.py:58
  3.7 0.5 fusion
  4.2 38.2 %all_to_all.20 = f16[8,64,2048]{2,1,0:T(8,128)(2,1)S(1)} all-to-all(f16[8,64,2048]{2,1,0:T(8,128)(2,1)S(1)} %fusion), channel_id=1, replica_groups={{0,64,128,192,256,320,384,448},{8,72,136,200,264,328,392,456},{16,80,14..., dimensions={0} | all-to-all | bytes 4194304 | tf_op jit(solution)/shard_map/all_to_all | solution.py:98
  42.4 0.5 convert_reduce_fusion
  42.9 12.5 %all_to_all.21 = f32[8,8,2048]{2,1,0:T(8,128)S(1)} all-to-all(f32[8,8,2048]{2,1,0:T(8,128)S(1)} %bitcast.7), channel_id=1, replica_groups={{0,16,32,48,8,24,40,56},{64,80,96,112,72,88,104,120},{128,144,160,176,1..., dimensions={0} | all-to-all | bytes 1048576 | tf_op jit(solution)/shard_map/all_to_all | solution.py:98
  55.5 10.2 %all_to_all.22 = bf16[4,8,2048]{2,1,0:T(8,128)(2,1)S(1)} all-to-all(bf16[4,8,2048]{2,1,0:T(8,128)(2,1)S(1)} %broadcast_in_dim.6), channel_id=1, replica_groups=mesh['pair'=2,'x'=4,'zh'=4,'zl'=2,'yh'=4,'core'=2] {'zh'}, dimensions={0} | all-to-all | bytes 262144 | tf_op jit(solution)/shard_map/all_to_all | solution.py:104
  65.7 0.1 broadcast_in_dim.7
  65.8 17.3 %all_to_all.23 = bf16[8,32,2048]{2,1,0:T(8,128)(2,1)S(1)} all-to-all(bf16[8,32,2048]{2,1,0:T(8,128)(2,1)S(1)} %broadcast_in_dim.7), channel_id=1, replica_groups=mesh['pair'=2,'x'=4,'zh'=4,'zl'=2,'yh'=4,'core'=2] {'x','zl'}, dimensions={0} | all-to-all | bytes 2097152 | tf_op jit(solution)/shard_map/all_to_all | solution.py:104
  83.1 1.0 %copy.4 = bf16[256,2048]{1,0:T(8,128)(2,1)} copy(bf16[256,2048]{1,0:T(8,128)(2,1)S(1)} %bitcast.6) | data formatting | bytes 2097152
  (3 shorter events, 0.0 us)

commit v8 on v6

v8 whole, which is shorter than its diff:
```python
import functools
import itertools
import math

import jax
import jax.numpy as jnp
from jax import lax
from jax.experimental import pallas as pl
from jax.experimental.pallas import tpu as pltpu
from jax.sharding import Mesh
from jax.sharding import PartitionSpec as P

SIZES = {"pair": 2, "x": 4, "zh": 4, "zl": 2}
TOKENS = ("pair", "x", "zh", "zl")
SLAB = ("yh", "core")
CORES = 2
SCALE = 2.0
CHUNKS = 2
PLANS = (
    {"sums": (("x", "zl"), ("pair", "zh")), "blocks": (2, 8), "order": (1, 0)},
    {"sums": (("pair", "zl"), ("x",), ("zh",)), "blocks": (2, 4, 2), "order": (0, 2, 1)},
)
GATHERS = (("zh",), ("x", "zl"))


def product_kernel(blocks, order, acts_hbm, cots_hbm, out, acts, cots, sems):
    cols = out.shape[-1]
    width = cols // CHUNKS
    loads = [pltpu.make_async_copy(acts_hbm, acts, sems.at[CHUNKS])]
    for i in range(CHUNKS):
        chunk = pl.ds(i * width, width)
        loads.append(pltpu.make_async_copy(cots_hbm.at[:, chunk], cots.at[:, chunk], sems.at[i]))
    for load in loads:
        load.start()
    loads[0].wait()
    for i in range(CHUNKS):
        loads[i + 1].wait()
        at = i * width
        part = lax.dot_general(
            acts[...],
            cots[:, at : at + width],
            (((0,), (0,)), ((), ())),
            preferred_element_type=jnp.float32,
        )
        rows = part.shape[0]
        piece = rows // math.prod(blocks)
        place = {}
        for n, index in enumerate(itertools.product(*(range(b) for b in blocks))):
            moved = 0
            for axis in order:
                moved = moved * blocks[axis] + index[axis]
            place[n] = moved
        for n, moved in place.items():
            out[moved * piece : (moved + 1) * piece, at : at + width] = part[
                n * piece : (n + 1) * piece
            ]


def product(activations, cotangents, plan):
    tokens, rows = activations.shape
    cols = cotangents.shape[1]
    return pl.pallas_call(
        functools.partial(product_kernel, plan["blocks"], plan["order"]),
        in_specs=[pl.BlockSpec(memory_space=pltpu.HBM)] * 2,
        out_specs=pl.BlockSpec(memory_space=pltpu.VMEM),
        out_shape=pltpu.VMEM((rows, cols), jnp.float32),
        scratch_shapes=[
            pltpu.VMEM((tokens, rows), activations.dtype),
            pltpu.VMEM((tokens, cols), cotangents.dtype),
            pltpu.SemaphoreType.DMA((CHUNKS + 1,)),
        ],
        compiler_params=pltpu.CompilerParams(vmem_limit_bytes=20 * 2**20),
        name="product",
    )(
        pltpu.with_memory_space_constraint(activations, pltpu.HBM),
        pltpu.with_memory_space_constraint(cotangents, pltpu.HBM),
    )


def groups(along):
    found = []
    for core in range(CORES):
        others = [axis for axis in SIZES if axis not in along]
        for rest in itertools.product(*(range(SIZES[axis]) for axis in others)):
            group = []
            for place in itertools.product(*(range(SIZES[axis]) for axis in along)):
                at = dict(zip((*others, *along), (*rest, *place)))
                z = at["zh"] * SIZES["zl"] + at["zl"] + core
                at["zh"], at["zl"] = divmod(z % (SIZES["zh"] * SIZES["zl"]), SIZES["zl"])
                index = 0
                for axis, size in SIZES.items():
                    index = index * size + at[axis]
                group.append(index * CORES + core)
            found.append(group)
    return found


def exchanged(x, along):
    return lax.all_to_all(
        x, (*SIZES, "core"), 0, 0, axis_index_groups=groups(along), tiled=True
    )


def peers(along):
    return math.prod(SIZES[axis] for axis in along)


def branch(plan):
    def run(activations, cotangents):
        cols = cotangents.shape[1]
        rows = (product(activations, cotangents, plan) * SCALE).astype(jnp.float16)
        for along in plan["sums"]:
            arrived = exchanged(rows.reshape(peers(along), -1, cols), along)
            rows = jnp.sum(arrived.astype(jnp.float32), axis=0)
        block = (rows * (1.0 / (SCALE * math.prod(SIZES.values())))).astype(jnp.bfloat16)
        for along in GATHERS:
            block = exchanged(jnp.broadcast_to(block, (peers(along), *block.shape)), along)
            block = block.reshape(-1, cols)
        return block

    return run


def local(activations, cotangents):
    first, second = (branch(plan) for plan in PLANS)
    return lax.cond(lax.axis_index("core") == 0, first, second, activations, cotangents)


def solution(mesh):
    split = Mesh(
        mesh.devices.reshape(*SIZES.values(), mesh.shape["ep"] // CORES, CORES),
        (*SIZES, *SLAB),
    )
    placed = (P(TOKENS, SLAB), P(TOKENS, SLAB))
    return jax.shard_map(
        local, mesh=split, in_specs=placed, out_specs=P("pair", SLAB), check_vma=False
    )
```

time: 83.4 us -> 83 us (level)
    all_to_all x4 -> x5, blocking collectives: 77.3 us -> 76.8 us  [exchanged(): lax.all_to_all(x, (*SIZES, 'core'), 0, 0, axis_index_groups=groups(along)...]
where the time goes in v8:
time: 83 us; the launch traced here: 82.8 us
  blocking collectives  76.8 us (93%)
  Pallas kernels  3.7 us (4%)
  other arithmetic  1.13 us (1%)
  local copies, waits for them, and re-layouts  1.09 us (1%)
    all_to_all x5, blocking collectives, exchanged(): lax.all_to_all(x, (*SIZES, 'core'), 0, 0, axis_index_groups=groups(along)...  76.8 us
    pallas_call x1, Pallas kernels, product(): pl.pallas_call(functools.partial(product_kernel, plan['blocks'], plan['or...  3.7 us

profile of v8, /device:TPU:1, one launch (start us, length us, event | category | flops | bytes accessed | tf_op | source)
XLA Modules:
  0.0 82.8 jit_solution(12766232552965607733)
XLA Ops:
  0.0 81.8 %conditional.1 = (bf16[256,2048]{1,0:T(8,128)(2,1)S(1)}) conditional(s32[]{:T(128)} %convert_element_type.21, (bf16[768,512]{1,0:T(8,128)(2,1)}, bf16[768,2048]{1,0:T(8,128)(2,1)}) %tuple.11, (bf16[768,512]{1,0:T(8,128)(2,1)}, bf16[768,2048]{1,0:T(8,128)(2,1)}) %tuple.11), branch_computations={%region_0.0_spmd, %region_4.0_spmd} | conditional | flops 4210688 | bytes 21692432 | solution.py:126
  0.0 3.7 %product.2 = f32[512,2048]{1,0:T(8,128)S(1)} custom-call(bf16[768,512]{1,0:T(8,128)(2,1)} %get-tuple-element.16.acts_hbm, bf16[768,2048]{1,0:T(8,128)(2,1)} %get-tuple-element.17.cots_hbm), custom_call_target="tpu_custom_call" | custom-call | tf_op jit(solution)/shard_map/cond/branch_0_fun/product/pallas_call | solution.py:62
  3.7 0.5 multiply_convert_fusion
  4.2 25.9 %all_to_all.36 = f16[4,128,2048]{2,1,0:T(8,128)(2,1)S(1)} all-to-all(f16[4,128,2048]{2,1,0:T(8,128)(2,1)S(1)} %bitcast.9), channel_id=1, replica_groups={{0,8,256,264},{16,24,272,280},{32,40,288,296},{48,56,304,312},{64,72,32..., dimensions={0} | all-to-all | bytes 4194304 | tf_op jit(solution)/shard_map/cond/branch_0_fun/all_to_all | solution.py:99
  30.2 0.5 convert_reduce_fusion
  30.7 13.3 %all_to_all.37 = f32[4,32,2048]{2,1,0:T(8,128)S(1)} all-to-all(f32[4,32,2048]{2,1,0:T(8,128)S(1)} %bitcast.11), channel_id=1, replica_groups={{0,64,128,192},{8,72,136,200},{16,80,144,208},{24,88,152,216},{32,96,16..., dimensions={0} | all-to-all | bytes 2097152 | tf_op jit(solution)/shard_map/cond/branch_0_fun/all_to_all | solution.py:99
  43.9 0.1 reduce_sum.41
  44.0 12.1 %all_to_all.38 = f32[4,8,2048]{2,1,0:T(8,128)S(1)} all-to-all(f32[4,8,2048]{2,1,0:T(8,128)S(1)} %bitcast.15), channel_id=1, replica_groups={{0,16,32,48},{8,24,40,56},{64,80,96,112},{72,88,104,120},{128,144,160,1..., dimensions={0} | all-to-all | bytes 524288 | tf_op jit(solution)/shard_map/cond/branch_0_fun/all_to_all | solution.py:99
  56.1 10.0 %all_to_all.39 = bf16[4,8,2048]{2,1,0:T(8,128)(2,1)S(1)} all-to-all(bf16[4,8,2048]{2,1,0:T(8,128)(2,1)S(1)} %broadcast_in_dim.8), channel_id=1, replica_groups={{0,16,32,48},{8,24,40,56},{64,80,96,112},{72,88,104,120},{128,144,160,1..., dimensions={0} | all-to-all | bytes 262144 | tf_op jit(solution)/shard_map/cond/branch_0_fun/all_to_all | solution.py:99
  66.1 0.1 broadcast_in_dim.9
  66.2 15.6 %all_to_all.40 = bf16[8,32,2048]{2,1,0:T(8,128)(2,1)S(1)} all-to-all(bf16[8,32,2048]{2,1,0:T(8,128)(2,1)S(1)} %broadcast_in_dim.9), channel_id=1, replica_groups={{0,8,64,72,128,136,192,200},{16,24,80,88,144,152,208,216},{32,40,96,104..., dimensions={0} | all-to-all | bytes 2097152 | tf_op jit(solution)/shard_map/cond/branch_0_fun/all_to_all | solution.py:99
  81.8 1.0 %copy.8 = bf16[256,2048]{1,0:T(8,128)(2,1)} copy(bf16[256,2048]{1,0:T(8,128)(2,1)S(1)} %get-tuple-element.20) | data formatting | bytes 2097152
  (3 shorter events, 0.0 us)

commit v9 on v8

--- a/solution.py
+++ b/solution.py
@@ -17,10 +17,21 @@
 SCALE = 2.0
 CHUNKS = 2
 PLANS = (
-    {"sums": (("x", "zl"), ("pair", "zh")), "blocks": (2, 8), "order": (1, 0)},
-    {"sums": (("pair", "zl"), ("x",), ("zh",)), "blocks": (2, 4, 2), "order": (0, 2, 1)},
+    {
+        "sums": (("x", "zl"), ("pair", "zh")),
+        "whole": (),
+        "gathers": (("zh",), ("x", "zl")),
+        "blocks": (2, 8),
+        "order": (1, 0),
+    },
+    {
+        "sums": (("pair", "zl"), ("x",)),
+        "whole": (("zh",),),
+        "gathers": (("x", "zl"),),
+        "blocks": (2, 4, 2),
+        "order": (0, 2, 1),
+    },
 )
-GATHERS = (("zh",), ("x", "zl"))
 
 
 def product_kernel(blocks, order, acts_hbm, cots_hbm, out, acts, cots, sems):
@@ -105,6 +116,10 @@
     return math.prod(SIZES[axis] for axis in along)
 
 
+def copies(x, along):
+    return exchanged(jnp.broadcast_to(x, (peers(along), *x.shape)), along)
+
+
 def branch(plan):
     def run(activations, cotangents):
         cols = cotangents.shape[1]
@@ -112,10 +127,11 @@
         for along in plan["sums"]:
             arrived = exchanged(rows.reshape(peers(along), -1, cols), along)
             rows = jnp.sum(arrived.astype(jnp.float32), axis=0)
+        for along in plan["whole"]:
+            rows = jnp.sum(copies(rows, along), axis=0)
         block = (rows * (1.0 / (SCALE * math.prod(SIZES.values())))).astype(jnp.bfloat16)
-        for along in GATHERS:
-            block = exchanged(jnp.broadcast_to(block, (peers(along), *block.shape)), along)
-            block = block.reshape(-1, cols)
+        for along in plan["gathers"]:
+            block = copies(block, along).reshape(-1, cols)
         return block
 
     return run

time: 83 us -> 84.5 us (1.018)
  blocking collectives: 76.8 us -> 77.8 us
    all_to_all x5 -> x4, blocking collectives: 76.8 us -> 77.8 us  [exchanged(): lax.all_to_all(x, (*SIZES, 'core'), 0, 0, axis_index_groups=groups(along)...]
where the time goes in v9:
time: 84.5 us; the launch traced here: 83.9 us
  blocking collectives  77.8 us (92%)
  Pallas kernels  3.7 us (4%)
  other arithmetic  1.19 us (1%)
  local copies, waits for them, and re-layouts  1.17 us (1%)
    all_to_all x4, blocking collectives, exchanged(): lax.all_to_all(x, (*SIZES, 'core'), 0, 0, axis_index_groups=groups(along)...  77.8 us
    pallas_call x1, Pallas kernels, product(): pl.pallas_call(functools.partial(product_kernel, plan['blocks'], plan['or...  3.7 us

profile of v9, /device:TPU:1, one launch (start us, length us, event | category | flops | bytes accessed | tf_op | source)
XLA Modules:
  0.0 83.9 jit_solution(17242279326155036434)
XLA Ops:
  0.0 82.9 %conditional.1 = (bf16[256,2048]{1,0:T(8,128)(2,1)S(1)}) conditional(s32[]{:T(128)} %convert_element_type.21, (bf16[768,512]{1,0:T(8,128)(2,1)}, bf16[768,2048]{1,0:T(8,128)(2,1)}) %tuple.11, (bf16[768,512]{1,0:T(8,128)(2,1)}, bf16[768,2048]{1,0:T(8,128)(2,1)}) %tuple.11), branch_computations={%region_0.0_spmd, %region_4.0_spmd} | conditional | flops 4456448 | bytes 25427984 | solution.py:142
  0.0 3.7 %product.2 = f32[512,2048]{1,0:T(8,128)S(1)} custom-call(bf16[768,512]{1,0:T(8,128)(2,1)} %get-tuple-element.16.acts_hbm, bf16[768,2048]{1,0:T(8,128)(2,1)} %get-tuple-element.17.cots_hbm), custom_call_target="tpu_custom_call" | custom-call | tf_op jit(solution)/shard_map/cond/branch_0_fun/product/pallas_call | solution.py:73
  3.7 0.5 multiply_convert_fusion
  4.2 25.9 %all_to_all.32 = f16[4,128,2048]{2,1,0:T(8,128)(2,1)S(1)} all-to-all(f16[4,128,2048]{2,1,0:T(8,128)(2,1)S(1)} %bitcast.7), channel_id=1, replica_groups={{0,8,256,264},{16,24,272,280},{32,40,288,296},{48,56,304,312},{64,72,32..., dimensions={0} | all-to-all | bytes 4194304 | tf_op jit(solution)/shard_map/cond/branch_0_fun/all_to_all | solution.py:110
  30.2 0.5 convert_reduce_fusion
  30.7 13.3 %all_to_all.33 = f32[4,32,2048]{2,1,0:T(8,128)S(1)} all-to-all(f32[4,32,2048]{2,1,0:T(8,128)S(1)} %bitcast.9), channel_id=1, replica_groups={{0,64,128,192},{8,72,136,200},{16,80,144,208},{24,88,152,216},{32,96,16..., dimensions={0} | all-to-all | bytes 2097152 | tf_op jit(solution)/shard_map/cond/branch_0_fun/all_to_all | solution.py:110
  43.9 0.1 reduce_sum.41
  44.0 0.1 broadcast_in_dim.8
  44.1 21.9 %all_to_all.34 = f32[4,32,2048]{2,1,0:T(8,128)S(1)} all-to-all(f32[4,32,2048]{2,1,0:T(8,128)S(1)} %broadcast_in_dim.8), channel_id=1, replica_groups={{0,16,32,48},{8,24,40,56},{64,80,96,112},{72,88,104,120},{128,144,160,1..., dimensions={0} | all-to-all | bytes 2097152 | tf_op jit(solution)/shard_map/cond/branch_0_fun/all_to_all | solution.py:110
  66.0 0.1 reduce_sum.42
  66.1 0.1 broadcast_in_dim.9
  66.2 16.7 %all_to_all.35 = bf16[8,32,2048]{2,1,0:T(8,128)(2,1)S(1)} all-to-all(bf16[8,32,2048]{2,1,0:T(8,128)(2,1)S(1)} %broadcast_in_dim.9), channel_id=1, replica_groups={{0,8,64,72,128,136,192,200},{16,24,80,88,144,152,208,216},{32,40,96,104..., dimensions={0} | all-to-all | bytes 2097152 | tf_op jit(solution)/shard_map/cond/branch_0_fun/all_to_all | solution.py:110
  82.9 1.0 %copy.8 = bf16[256,2048]{1,0:T(8,128)(2,1)} copy(bf16[256,2048]{1,0:T(8,128)(2,1)S(1)} %get-tuple-element.20) | data formatting | bytes 2097152
  (1 shorter events, 0.0 us)

commit v10 on v8

--- a/solution.py
+++ b/solution.py
@@ -17,10 +17,9 @@
 SCALE = 2.0
 CHUNKS = 2
 PLANS = (
-    {"sums": (("x", "zl"), ("pair", "zh")), "blocks": (2, 8), "order": (1, 0)},
-    {"sums": (("pair", "zl"), ("x",), ("zh",)), "blocks": (2, 4, 2), "order": (0, 2, 1)},
+    {"sums": (("x", "zl"), ("pair", "zh")), "blocks": (2, 8), "order": (1, 0), "gathers": (("zh",), ("x", "zl"))},
+    {"sums": (("pair", "zl"), ("x",), ("zh",)), "blocks": (2, 4, 2), "order": (0, 2, 1), "gathers": (("zl", "zh"), ("x",))},
 )
-GATHERS = (("zh",), ("x", "zl"))
 
 
 def product_kernel(blocks, order, acts_hbm, cots_hbm, out, acts, cots, sems):
@@ -113,7 +112,7 @@
             arrived = exchanged(rows.reshape(peers(along), -1, cols), along)
             rows = jnp.sum(arrived.astype(jnp.float32), axis=0)
         block = (rows * (1.0 / (SCALE * math.prod(SIZES.values())))).astype(jnp.bfloat16)
-        for along in GATHERS:
+        for along in plan["gathers"]:
             block = exchanged(jnp.broadcast_to(block, (peers(along), *block.shape)), along)
             block = block.reshape(-1, cols)
         return block

time: 83 us -> 83 us (level)
  no operation moved by 1% of the time
where the time goes in v10:
time: 83 us; the launch traced here: 82.8 us
  blocking collectives  76.8 us (93%)
  Pallas kernels  3.7 us (4%)
  other arithmetic  1.13 us (1%)
  local copies, waits for them, and re-layouts  1.1 us (1%)
    all_to_all x5, blocking collectives, exchanged(): lax.all_to_all(x, (*SIZES, 'core'), 0, 0, axis_index_groups=groups(along)...  76.8 us
    pallas_call x1, Pallas kernels, product(): pl.pallas_call(functools.partial(product_kernel, plan['blocks'], plan['or...  3.7 us

profile of v10, /device:TPU:1, one launch (start us, length us, event | category | flops | bytes accessed | tf_op | source)
XLA Modules:
  0.0 82.8 jit_solution(993167327385299061)
XLA Ops:
  0.0 81.8 %conditional.1 = (bf16[256,2048]{1,0:T(8,128)(2,1)S(1)}) conditional(s32[]{:T(128)} %convert_element_type.21, (bf16[768,512]{1,0:T(8,128)(2,1)}, bf16[768,2048]{1,0:T(8,128)(2,1)}) %tuple.11, (bf16[768,512]{1,0:T(8,128)(2,1)}, bf16[768,2048]{1,0:T(8,128)(2,1)}) %tuple.11), branch_computations={%region_0.0_spmd, %region_4.0_spmd} | conditional | flops 4210688 | bytes 22216720 | solution.py:125
  0.0 3.7 %product.2 = f32[512,2048]{1,0:T(8,128)S(1)} custom-call(bf16[768,512]{1,0:T(8,128)(2,1)} %get-tuple-element.16.acts_hbm, bf16[768,2048]{1,0:T(8,128)(2,1)} %get-tuple-element.17.cots_hbm), custom_call_target="tpu_custom_call" | custom-call | tf_op jit(solution)/shard_map/cond/branch_0_fun/product/pallas_call | solution.py:61
  3.7 0.5 multiply_convert_fusion
  4.2 25.9 %all_to_all.36 = f16[4,128,2048]{2,1,0:T(8,128)(2,1)S(1)} all-to-all(f16[4,128,2048]{2,1,0:T(8,128)(2,1)S(1)} %bitcast.9), channel_id=1, replica_groups={{0,8,256,264},{16,24,272,280},{32,40,288,296},{48,56,304,312},{64,72,32..., dimensions={0} | all-to-all | bytes 4194304 | tf_op jit(solution)/shard_map/cond/branch_0_fun/all_to_all | solution.py:98
  30.2 0.5 convert_reduce_fusion
  30.7 13.3 %all_to_all.37 = f32[4,32,2048]{2,1,0:T(8,128)S(1)} all-to-all(f32[4,32,2048]{2,1,0:T(8,128)S(1)} %bitcast.11), channel_id=1, replica_groups={{0,64,128,192},{8,72,136,200},{16,80,144,208},{24,88,152,216},{32,96,16..., dimensions={0} | all-to-all | bytes 2097152 | tf_op jit(solution)/shard_map/cond/branch_0_fun/all_to_all | solution.py:98
  43.9 0.1 reduce_sum.41
  44.0 12.1 %all_to_all.38 = f32[4,8,2048]{2,1,0:T(8,128)S(1)} all-to-all(f32[4,8,2048]{2,1,0:T(8,128)S(1)} %bitcast.15), channel_id=1, replica_groups={{0,16,32,48},{8,24,40,56},{64,80,96,112},{72,88,104,120},{128,144,160,1..., dimensions={0} | all-to-all | bytes 524288 | tf_op jit(solution)/shard_map/cond/branch_0_fun/all_to_all | solution.py:98
  56.1 11.5 %all_to_all.39 = bf16[8,8,2048]{2,1,0:T(8,128)(2,1)S(1)} all-to-all(bf16[8,8,2048]{2,1,0:T(8,128)(2,1)S(1)} %broadcast_in_dim.8), channel_id=1, replica_groups={{0,16,32,48,8,24,40,56},{64,80,96,112,72,88,104,120},{128,144,160,176,1..., dimensions={0} | all-to-all | bytes 524288 | tf_op jit(solution)/shard_map/cond/branch_0_fun/all_to_all | solution.py:98
  67.6 0.1 broadcast_in_dim.9
  67.8 14.0 %all_to_all.40 = bf16[4,64,2048]{2,1,0:T(8,128)(2,1)S(1)} all-to-all(bf16[4,64,2048]{2,1,0:T(8,128)(2,1)S(1)} %broadcast_in_dim.9), channel_id=1, replica_groups={{0,64,128,192},{8,72,136,200},{16,80,144,208},{24,88,152,216},{32,96,16..., dimensions={0} | all-to-all | bytes 2097152 | tf_op jit(solution)/shard_map/cond/branch_0_fun/all_to_all | solution.py:98
  81.8 1.0 %copy.8 = bf16[256,2048]{1,0:T(8,128)(2,1)} copy(bf16[256,2048]{1,0:T(8,128)(2,1)S(1)} %get-tuple-element.20) | data formatting | bytes 2097152
  (3 shorter events, 0.0 us)
